TPU v7x, 32 devices: a whole 2x2x4 slice. The times are simulated.
32 devices in a mesh: rep: 4 (over y, core), shard: 8 (over z, x).
Axes of the slice: x: 2, y: 2, z: 4, core: 2. Of those that a mesh axis runs over, the one named last changes fastest.
Arguments:
- hidden: bfloat16 [14336, 3584], P(('rep', 'shard')), may hold values from -144 to 144
- cotangent: bfloat16 [14336, 1024], P(('rep', 'shard')), may hold values from -6 to 6
- seq_ids: int32 [32, 448], P(('rep', 'shard')), may hold values from 0 to 3, as said below
- response_mask: int32 [32, 448], P(('rep', 'shard')), may hold values from 0 to 1, as said below
- group_ids: int32 [32, 4], P(('rep', 'shard')), may hold values from 0 to 15
- rewards: float32 [32, 4], P(('rep', 'shard')), may hold values from -6 to 6
- new_logp: float32 [32, 448], P(('rep', 'shard')), may hold values from -1.5 to -0.1
- old_logp: float32 [32, 448], P(('rep', 'shard')), may hold values from -1.5 to -0.1
- ref_logp: float32 [32, 448], P(('rep', 'shard')), may hold values from -1.5 to -0.1
- master: float32 [3, 3584, 1024], P(None, 'shard'), may hold values from -6 to 6
Outputs:
- new_master: float32 [3584, 1024], P('shard')
- rollout: bfloat16 [3, 3584, 2048], P(None, None, 'shard')
Inputs may be any that keep to these rules, and one draw needn't show every extreme that they name: `seq_ids`: each row numbers its device's 4 sequences in token order, never falling, each with one token or more. `response_mask`: within a sequence, prompt tokens come before response tokens; a sequence may have no response tokens.
All inputs are finite; a program needn't handle non-finite values.
Results may differ from a plain program's by a relative error of at most 0.0095.
Values may be sent and summed in bfloat16 or wider, within the bound.
A program may use at most 128 MiB of HBM per device.

v0:
```python
import jax
import jax.numpy as jnp
from jax import lax
from jax.sharding import PartitionSpec as P

HEAD = 128
KV_HEADS = 4
TP = 8
SEQ_DEV = 4


def token_coef(seq_row, mask_row, adv_row, new_row, old_row, ref_row):
    onehot = (seq_row[:, None] == jnp.arange(SEQ_DEV, dtype=jnp.int32)[None, :]).astype(jnp.float32)
    maskf = mask_row.astype(jnp.float32)
    lengths = jnp.maximum(jnp.dot(maskf, onehot, precision=lax.Precision.HIGHEST), 1.0)
    tok_len = jnp.dot(onehot, lengths, precision=lax.Precision.HIGHEST)
    tok_adv = jnp.dot(onehot, adv_row, precision=lax.Precision.HIGHEST)
    surrogate = -tok_adv * jnp.exp(new_row - old_row) + 0.2 * (1.0 - jnp.exp(ref_row - new_row))
    return maskf / tok_len * surrogate


def group_advantage(group_flat, reward_flat, stats):
    groups = stats.shape[1]
    onehot = (group_flat[:, None] == jnp.arange(groups, dtype=jnp.int32)[None, :]).astype(
        jnp.float32
    )
    count = jnp.maximum(stats[0], 1.0)
    mean = stats[1] / count
    spread = jnp.sqrt(jnp.maximum(stats[2] / count - mean * mean, 0.0))
    tok_mean = jnp.dot(onehot, mean, precision=lax.Precision.HIGHEST)
    tok_std = jnp.dot(onehot, jnp.maximum(spread, 0.5), precision=lax.Precision.HIGHEST)
    return (reward_flat - tok_mean) / tok_std


def group_sums(group_flat, reward_flat, groups):
    onehot = (group_flat[:, None] == jnp.arange(groups, dtype=jnp.int32)[None, :]).astype(
        jnp.float32
    )
    values = jnp.stack([jnp.ones_like(reward_flat), reward_flat, reward_flat * reward_flat], axis=0)
    return jnp.dot(values, onehot, precision=lax.Precision.HIGHEST)


def rounded(term):
    return lax.optimization_barrier(term.astype(jnp.bfloat16)).astype(jnp.float32)


def rollout_blocks(weights):
    layer_count = weights.shape[0]
    row_count = weights.shape[1]
    paired = weights.reshape(layer_count, row_count, 2, KV_HEADS, HEAD).transpose(0, 1, 3, 2, 4)
    paired = paired.reshape(layer_count, row_count, KV_HEADS, 2 * HEAD)
    by_rank = jnp.repeat(paired, TP // KV_HEADS, axis=2)
    copies = jnp.tile(by_rank, (1, 1, lax.axis_size("shard") // TP, 1))
    return copies.reshape(layer_count, row_count, lax.axis_size("shard") * 2 * HEAD)


def per_device(
    hidden,
    cotangent,
    seq_ids,
    response_mask,
    group_ids,
    rewards,
    new_logp,
    old_logp,
    ref_logp,
    master,
):
    n_rep = lax.axis_size("rep")
    n_shard = lax.axis_size("shard")
    groups = n_rep * n_shard * SEQ_DEV // 8
    rest_cols = lax.all_to_all(
        rollout_blocks(master[1:].astype(jnp.bfloat16)),
        "shard",
        split_axis=2,
        concat_axis=1,
        tiled=True,
    )
    local_sums = group_sums(group_ids[0], rewards[0], groups)
    stats = lax.psum(local_sums, ("rep", "shard"))
    advantage = group_advantage(group_ids[0], rewards[0], stats)
    coef = token_coef(
        seq_ids[0], response_mask[0], advantage, new_logp[0], old_logp[0], ref_logp[0]
    )
    delta = (coef[:, None] * cotangent.astype(jnp.float32)).astype(jnp.bfloat16)
    feature_count = hidden.shape[1]
    partial_value = lax.psum_scatter(
        rounded(
            lax.dot_general(
                hidden, delta, (((0,), (0,)), ((), ())), preferred_element_type=jnp.float32
            )
        ).astype(jnp.bfloat16),
        "shard",
        scatter_dimension=0,
        tiled=True,
    )
    grad = lax.psum(partial_value, "rep").astype(jnp.float32)
    squares = lax.psum(jnp.sum(grad * grad), "shard")
    rms = jnp.sqrt(squares / (feature_count * grad.shape[1]) + 1e-06)
    new_master = master[0] - 0.5 * grad / rms
    first_cols = lax.all_to_all(
        rollout_blocks(new_master[None].astype(jnp.bfloat16)),
        "shard",
        split_axis=2,
        concat_axis=1,
        tiled=True,
    )
    rollout = jnp.concatenate([first_cols, rest_cols], axis=0)
    return (new_master, rollout)


def solution(mesh):
    in_specs = (
        P(("rep", "shard"), None),
        P(("rep", "shard"), None),
        P(("rep", "shard"), None),
        P(("rep", "shard"), None),
        P(("rep", "shard"), None),
        P(("rep", "shard"), None),
        P(("rep", "shard"), None),
        P(("rep", "shard"), None),
        P(("rep", "shard"), None),
        P(None, "shard", None),
    )
    out_specs = (P("shard", None), P(None, None, "shard"))
    return jax.shard_map(
        per_device, mesh=mesh, in_specs=in_specs, out_specs=out_specs, check_vma=False
    )
```

profile of v0, /device:TPU:0, one launch (start us, length us, event | category | flops | bytes accessed | tf_op | source)
XLA Modules:
  0.0 468.4 jit_solution(8274017862780211825)
XLA Ops:
  9.0 41.9 %psum.21 = f32[3,16]{1,0:T(4,128)S(1)} all-reduce(f32[3,16]{1,0:T(4,128)S(1)} %fusion.15), channel_id=1, replica_groups=mesh['rep'=4,'shard'=8] {'rep','shard'}, use_global_device_ids=true, to_apply=%region_0.0 | all-reduce | flops 48 | bytes 384 | tf_op jit(solution)/shard_map/psum | solution.py:80
  55.3 1.0 fusion.11
  57.1 7.5 %fusion = bf16[3584,1024]{0,1:T(8,128)(2,1)} fusion(bf16[448,3584]{1,0:T(8,128)(2,1)S(1)} %copy-done, bf16[448,1024]{1,0:T(8,128)(2,1)} %param.11, f32[448]{0:T(512)S(1)} %add_multiply_fusion), kind=kOutput, calls=%fused_computation.1 | convolution fusion | flops 3293380608 | bytes 11470592 | tf_op jit(solution)/shard_map/dot_general | solution.py:89
  64.6 10.4 %copy.47 = bf16[3584,1024]{1,0:T(8,128)(2,1)} copy(bf16[3584,1024]{0,1:T(8,128)(2,1)} %fusion) | data formatting | bytes 14680064
  75.0 2.3 slice.36
  77.4 2.3 reshape.41
  79.6 5.7 %copy.49 = bf16[2,448,2,4,128]{1,0,4,2,3:T(2,128)(2,1)S(1)} copy(bf16[2,448,2,4,128]{4,3,2,1,0:T(4,128)(2,1)} %reshape.41) | data formatting | bytes 3670016 | tf_op jit(solution)/shard_map/transpose | solution.py:50
  85.3 4.2 broadcast_in_dim.15
  89.5 5.3 %all-to-all-start.1 = ((bf16[2,448,2048]{1,0,2:T(2,128)(2,1)}), bf16[2,448,2048]{1,0,2:T(2,128)(2,1)}, u32[]{:S(2)}, u32[]{:S(2)}) async-start(bf16[2,448,2048]{1,0,2:T(2,128)(2,1)} %bitcast.83), calls=%async_computation.1 | async-start | bytes 8388608 | tf_op jit(solution)/shard_map/all_to_all | solution.py:72
  94.9 188.3 %reduce-scatter.4.cloned.1.call-done = bf16[448,1024]{1,0:T(8,128)(2,1)} async-done(((bf16[3584,1024]{1,0:T(8,128)(2,1)}), bf16[448,1024]{1,0:T(8,128)(2,1)}) %reduce-scatter.4.cloned.1.call-update) | async-done | bytes 917520
  283.2 2.2 copy.48
  285.4 36.1 %all-reduce.2.cloned.1.call-done = bf16[448,1024]{0,1:T(8,128)(2,1)} async-done(((bf16[448,1024]{0,1:T(8,128)(2,1)}), bf16[448,1024]{0,1:T(8,128)(2,1)}) %all-reduce.2.cloned.1.call-update) | async-done | bytes 917520 | tf_op jit(solution)/shard_map/psum | solution.py:97
  321.5 2.4 fusion.3
  323.9 1.9 copy.51
  325.7 22.1 %psum.23 = f32[]{:T(128)} all-reduce(f32[]{:T(128)} %fusion.3), channel_id=1, replica_groups=mesh['rep'=4,'shard'=8] {'shard'}, use_global_device_ids=true, to_apply=%region_4.0 | all-reduce | flops 1 | bytes 8 | tf_op jit(solution)/shard_map/psum | solution.py:98
  348.6 3.0 fusion.36
  351.6 3.6 copy.33
  355.2 2.7 reshape.40
  358.6 2.5 broadcast_in_dim.6
  361.1 5.3 %broadcast_in_dim.14 = bf16[1,448,2048]{2,1,0:T(8,128)(2,1)} reshape(bf16[448,4,2,256]{3,2,1,0:T(2,128)(2,1)} %broadcast_in_dim.6) | data formatting | bytes 3670016 | tf_op jit(solution)/shard_map/broadcast_in_dim | solution.py:52
  366.4 10.7 %copy.35 = bf16[1,448,2048]{1,0,2:T(2,128)(2,1)} copy(bf16[1,448,2048]{2,1,0:T(8,128)(2,1)} %broadcast_in_dim.14) | data formatting | bytes 3670016 | tf_op jit(solution)/shard_map/broadcast_in_dim | solution.py:52
  377.6 15.4 %reduce = bf16[2048,448]{1,0:T(8,128)(2,1)} reduce(bf16[2048,1,448]{2,1,0:T(2,128)(2,1)} %bitcast.84, bf16[]{:T(256)} %broadcast.50), dimensions={1}, to_apply=%bitcast.77.reduce_sub_computation | reduce | bytes 3670018
  393.1 6.8 %reshape.57 = bf16[8,2,57344]{2,1,0:T(2,128)(2,1)} reshape(bf16[2048,448]{1,0:T(8,128)(2,1)} %reduce) | data formatting | bytes 3670016
  399.8 4.3 all-to-all-start
  404.2 11.1 %copy.46 = bf16[2,448,8,256]{3,1,2,0:T(8,128)(2,1)} copy(bf16[2,448,8,256]{1,0,3,2:T(2,128)(2,1)} %bitcast.27) | data formatting | bytes 7340032 | tf_op jit(solution)/shard_map/all_to_all | solution.py:72
  415.3 1.7 copy.42
  417.0 25.9 %all-to-all-done = bf16[8,2,57344]{2,1,0:T(2,128)(2,1)} async-done(((bf16[8,2,57344]{2,1,0:T(2,128)(2,1)}), bf16[8,2,57344]{2,1,0:T(2,128)(2,1)}, u32[]{:S(2)}, u32[]{:S(2)}) %all-to-all-start) | async-done | bytes 1835040 | tf_op jit(solution)/shard_map/all_to_all | solution.py:101
  442.9 7.2 %reshape.58 = bf16[2048,1,448]{2,1,0:T(2,128)(2,1)} reshape(bf16[8,2,57344]{2,1,0:T(2,128)(2,1)} %all-to-all-done) | data formatting | bytes 3670016
  450.1 2.8 copy.50
  452.9 3.0 copy.43
  455.8 2.0 copy.37
  458.4 2.9 pad_maximum_fusion
  (28 shorter events, 9.0 us)
Async XLA Ops:
  7.2 49.9 %copy-start = (bf16[448,3584]{1,0:T(8,128)(2,1)S(1)}, bf16[448,3584]{1,0:T(8,128)(2,1)}, u32[]{:S(2)}) copy-start(bf16[448,3584]{1,0:T(8,128)(2,1)} %param.10) | copy-start | bytes 9633796
  7.2 276.0 %reduce-scatter.4.cloned.1.call-start = ((), (), s32[]{:S(2)}) async-start(), calls=%async_computation.4 | async-start | bytes 8257536
  89.5 310.4 %all-to-all-start.1 = ((bf16[2,448,2048]{1,0,2:T(2,128)(2,1)}), bf16[2,448,2048]{1,0,2:T(2,128)(2,1)}, u32[]{:S(2)}, u32[]{:S(2)}) async-start(bf16[2,448,2048]{1,0,2:T(2,128)(2,1)} %bitcast.83), calls=%async_computation.1 | async-start | bytes 8388608 | tf_op jit(solution)/shard_map/all_to_all | solution.py:72
  94.8 226.7 %all-reduce.2.cloned.1.call-start = ((), (), s32[]{:S(2)}) async-start(), calls=%async_computation.3 | async-start | bytes 2097152 | tf_op jit(solution)/shard_map/psum | solution.py:97
  285.4 38.5 %slice-start = ((f32[3,448,1024]{2,1,0:T(8,128)}), f32[1,448,1024]{2,1,0:T(8,128)S(1)}, s32[]{:S(2)}) async-start(f32[3,448,1024]{2,1,0:T(8,128)} %param.19), calls=%async_computation.5 | async-start | bytes 3670016 | tf_op jit(solution)/shard_map/slice | solution.py:100
  323.9 24.7 %copy-start.3 = (bf16[448,1024]{0,1:T(8,128)(2,1)S(1)}, bf16[448,1024]{0,1:T(8,128)(2,1)}, u32[]{:S(2)}) copy-start(bf16[448,1024]{0,1:T(8,128)(2,1)} %all-reduce.2.cloned.1.call-done) | copy-start | bytes 2752516
  399.8 43.1 %all-to-all-start = ((bf16[8,2,57344]{2,1,0:T(2,128)(2,1)}), bf16[8,2,57344]{2,1,0:T(2,128)(2,1)}, u32[]{:S(2)}, u32[]{:S(2)}) async-start(bf16[8,2,57344]{2,1,0:T(2,128)(2,1)} %reshape.57), calls=%async_computation | async-start | bytes 3670016 | tf_op jit(solution)/shard_map/all_to_all | solution.py:101
  455.8 2.6 copy-start.2
  458.4 3.1 copy-start.1
Sparse Core Ops, SparseCore 0:
  75.2 207.9 reduce-scatter.3
  286.1 35.3 all-reduce.1
where the time goes:
time: 470 us; the launch traced here: 468 us
  waiting for transfers between devices  250 us (53%)
  local copies, waits for them, and re-layouts  90.3 us (19%)
  blocking collectives  64.1 us (14%)
  other arithmetic  26 us (6%)
  between operations  14.8 us (3%)
  matrix products  13.1 us (3%)
  starting transfers between devices  9.74 us (2%)
    unnamed x3, waiting for transfers between devices  188 us
    psum x1, blocking collectives, per_device(): stats = lax.psum(local_sums, ('rep', 'shard'))  41.9 us
    psum x1, waiting for transfers between devices, per_device(): grad = lax.psum(partial_value, 'rep').astype(jnp.float32)  36.1 us
    unnamed x16, local copies, waits for them, and re-layouts  34.2 us
    all_to_all x1, waiting for transfers between devices, per_device(): lax.all_to_all(rollout_blocks(new_master[None].astype(jnp.bfloat16)), 'sh...  25.9 us
    broadcast_in_dim x4, local copies, waits for them, and re-layouts, rollout_blocks(): by_rank = jnp.repeat(paired, TP // KV_HEADS, axis=2)  22.7 us
    psum x1, blocking collectives, per_device(): squares = lax.psum(jnp.sum(grad * grad), 'shard')  22.1 us
    unnamed x1, other arithmetic  15.4 us
  transfers between devices with their start and end apart: 4, of which 3 were waited for; matrix products, arithmetic and copies ran while one was open for 18% of the time, Pallas kernels for 0%

commit v1 on v0

--- a/solution.py
+++ b/solution.py
@@ -94,7 +94,7 @@
         scatter_dimension=0,
         tiled=True,
     )
-    grad = lax.psum(partial_value, "rep").astype(jnp.float32)
+    grad = jnp.sum(lax.all_gather(partial_value, "rep"), axis=0).astype(jnp.float32)
     squares = lax.psum(jnp.sum(grad * grad), "shard")
     rms = jnp.sqrt(squares / (feature_count * grad.shape[1]) + 1e-06)
     new_master = master[0] - 0.5 * grad / rms

time: 470 us -> 448 us (0.953)
  local copies, waits for them, and re-layouts: 90.3 us -> 71.1 us
    reduce_scatter x0 -> x1, waiting for transfers between devices: none -> 188 us  [per_device(): lax.psum_scatter(rounded(lax.dot_general(hidden, delta, (((0,), (0,)), ((...]
    unnamed x3 -> x2, waiting for transfers between devices: 188 us -> 0.03 us
    psum x1 -> x0, waiting for transfers between devices: 36.1 us -> none  [per_device(): grad = lax.psum(partial_value, 'rep').astype(jnp.float32)]
    all_gather x0 -> x1, waiting for transfers between devices: none -> 32.1 us  [per_device(): lax.all_gather(partial_value, 'rep')]
    unnamed x16 -> x11, local copies, waits for them, and re-layouts: 34.2 us -> 23.7 us
  transfers between devices with their start and end apart: 4 -> 4, of which waited for: 3 -> 3; matrix products, arithmetic and copies ran while one was open for 18% -> 16% of each run, Pallas kernels for 0% -> 0%
where the time goes in v1:
time: 448 us; the launch traced here: 446 us
  waiting for transfers between devices  246 us (55%)
  local copies, waits for them, and re-layouts  71.1 us (16%)
  blocking collectives  64.1 us (14%)
  other arithmetic  28.3 us (6%)
  between operations  14.9 us (3%)
  matrix products  13.2 us (3%)
  starting transfers between devices  9.02 us (2%)
    reduce_scatter x1, waiting for transfers between devices, per_device(): lax.psum_scatter(rounded(lax.dot_general(hidden, delta, (((0,), (0,)), ((...  188 us
    psum x1, blocking collectives, per_device(): stats = lax.psum(local_sums, ('rep', 'shard'))  41.9 us
    all_gather x1, waiting for transfers between devices, per_device(): lax.all_gather(partial_value, 'rep')  32.1 us
    all_to_all x1, waiting for transfers between devices, per_device(): lax.all_to_all(rollout_blocks(new_master[None].astype(jnp.bfloat16)), 'sh...  25.4 us
    unnamed x11, local copies, waits for them, and re-layouts  23.7 us
    psum x1, blocking collectives, per_device(): squares = lax.psum(jnp.sum(grad * grad), 'shard')  22.1 us
    broadcast_in_dim x4, local copies, waits for them, and re-layouts, rollout_blocks(): by_rank = jnp.repeat(paired, TP // KV_HEADS, axis=2)  18.4 us
    unnamed x1, other arithmetic  14.1 us
  transfers between devices with their start and end apart: 4, of which 3 were waited for; matrix products, arithmetic and copies ran while one was open for 16% of the time, Pallas kernels for 0%

profile of v1, /device:TPU:0, one launch (start us, length us, event | category | flops | bytes accessed | tf_op | source)
XLA Modules:
  0.0 446.5 jit_solution(1976028733505066821)
XLA Ops:
  8.1 1.0 fusion.15
  9.0 41.9 %psum.14 = f32[3,16]{1,0:T(4,128)S(1)} all-reduce(f32[3,16]{1,0:T(4,128)S(1)} %fusion.15), channel_id=1, replica_groups=mesh['rep'=4,'shard'=8] {'rep','shard'}, use_global_device_ids=true, to_apply=%region_0.0 | all-reduce | flops 48 | bytes 384 | tf_op jit(solution)/shard_map/psum | solution.py:80
  53.4 0.9 fusion.5
  54.3 1.0 fusion.10
  55.3 1.0 fusion.11
  57.1 7.5 %fusion = bf16[3584,1024]{0,1:T(8,128)(2,1)} fusion(bf16[448,3584]{1,0:T(8,128)(2,1)S(1)} %copy-done, bf16[448,1024]{1,0:T(8,128)(2,1)} %param.11, f32[448]{0:T(512)S(1)} %add_multiply_fusion), kind=kOutput, calls=%fused_computation.1 | convolution fusion | flops 3293380608 | bytes 11470592 | tf_op jit(solution)/shard_map/dot_general | solution.py:89
  64.7 10.4 %copy.35 = bf16[3584,1024]{1,0:T(8,128)(2,1)} copy(bf16[3584,1024]{0,1:T(8,128)(2,1)} %fusion) | data formatting | bytes 14680064
  75.1 2.3 slice.38
  77.4 2.3 reshape.58
  79.7 5.7 %copy.37 = bf16[2,448,2,4,128]{1,0,4,2,3:T(2,128)(2,1)S(1)} copy(bf16[2,448,2,4,128]{4,3,2,1,0:T(4,128)(2,1)} %reshape.58) | data formatting | bytes 3670016 | tf_op jit(solution)/shard_map/transpose | solution.py:50
  85.3 4.2 broadcast_in_dim.15
  89.5 5.3 %all-to-all-start.1 = ((bf16[2,448,2048]{1,0,2:T(2,128)(2,1)}), bf16[2,448,2048]{1,0,2:T(2,128)(2,1)}, u32[]{:S(2)}, u32[]{:S(2)}) async-start(bf16[2,448,2048]{1,0,2:T(2,128)(2,1)} %bitcast.88), calls=%async_computation.1 | async-start | bytes 8388608 | tf_op jit(solution)/shard_map/all_to_all | solution.py:72
  94.9 188.3 %reduce-scatter.4.cloned.1.call-done = bf16[448,1024]{1,0:T(8,128)(2,1)} async-done(((bf16[3584,1024]{1,0:T(8,128)(2,1)}), bf16[448,1024]{1,0:T(8,128)(2,1)}) %reduce-scatter.4.cloned.1.call-update) | async-done | bytes 917520 | tf_op jit(solution)/shard_map/reduce_scatter | solution.py:87
  283.3 32.1 %all-gather.3.cloned.1.call-done = bf16[1792,1024]{1,0:T(8,128)(2,1)} async-done(((bf16[448,1024]{1,0:T(8,128)(2,1)}), bf16[1792,1024]{1,0:T(8,128)(2,1)}) %all-gather.3.cloned.1.call-update) | async-done | bytes 3670032 | tf_op jit(solution)/shard_map/all_gather | solution.py:97
  315.4 2.9 reduce_sum.21
  318.3 1.1 fusion.2
  319.4 22.1 %psum.15 = f32[]{:T(128)} all-reduce(f32[]{:T(128)} %fusion.2), channel_id=1, replica_groups=mesh['rep'=4,'shard'=8] {'shard'}, use_global_device_ids=true, to_apply=%region_4.0 | all-reduce | flops 1 | bytes 8 | tf_op jit(solution)/shard_map/psum | solution.py:98
  342.2 1.8 fusion.3
  346.8 1.3 broadcast_in_dim.6
  348.1 2.3 broadcast_in_dim.14
  350.4 10.7 %copy.24 = bf16[1,448,2048]{1,0,2:T(2,128)(2,1)} copy(bf16[1,448,2048]{2,1,0:T(8,128)(2,1)} %broadcast_in_dim.14) | data formatting | bytes 3670016 | tf_op jit(solution)/shard_map/broadcast_in_dim | solution.py:52
  361.6 14.1 %reduce.1 = bf16[2048,448]{1,0:T(8,128)(2,1)S(1)} reduce(bf16[2048,1,448]{2,1,0:T(2,128)(2,1)} %bitcast.89, bf16[]{:T(256)} %broadcast.68), dimensions={1}, to_apply=%bitcast.82.reduce_sub_computation | reduce | bytes 3670018
  375.7 4.4 reshape.75
  380.1 3.6 all-to-all-start
  383.7 11.1 %copy.34 = bf16[2,448,8,256]{3,1,2,0:T(8,128)(2,1)} copy(bf16[2,448,8,256]{1,0,3,2:T(2,128)(2,1)} %bitcast.28) | data formatting | bytes 7340032 | tf_op jit(solution)/shard_map/all_to_all | solution.py:72
  394.9 3.2 bitcast_subtract_fusion.1
  398.0 25.4 %all-to-all-done = bf16[8,2,57344]{2,1,0:T(2,128)(2,1)S(1)} async-done(((bf16[8,2,57344]{2,1,0:T(2,128)(2,1)}), bf16[8,2,57344]{2,1,0:T(2,128)(2,1)S(1)}, u32[]{:S(2)}, u32[]{:S(2)}) %all-to-all-start) | async-done | bytes 1835040 | tf_op jit(solution)/shard_map/all_to_all | solution.py:101
  423.4 4.8 %reshape.76 = bf16[2048,1,448]{2,1,0:T(2,128)(2,1)} reshape(bf16[8,2,57344]{2,1,0:T(2,128)(2,1)S(1)} %all-to-all-done) | data formatting | bytes 3670016
  428.2 2.8 copy.38
  431.0 3.0 copy.31
  434.0 2.0 copy.26
  436.6 2.9 pad_maximum_fusion
  (24 shorter events, 8.1 us)
Async XLA Ops:
  7.2 49.9 %copy-start = (bf16[448,3584]{1,0:T(8,128)(2,1)S(1)}, bf16[448,3584]{1,0:T(8,128)(2,1)}, u32[]{:S(2)}) copy-start(bf16[448,3584]{1,0:T(8,128)(2,1)} %param.10) | copy-start | bytes 9633796
  7.2 276.1 %reduce-scatter.4.cloned.1.call-start = ((), (), s32[]{:S(2)}) async-start(), calls=%async_computation.4 | async-start | bytes 8257536 | tf_op jit(solution)/shard_map/reduce_scatter | solution.py:87
  89.5 290.6 %all-to-all-start.1 = ((bf16[2,448,2048]{1,0,2:T(2,128)(2,1)}), bf16[2,448,2048]{1,0,2:T(2,128)(2,1)}, u32[]{:S(2)}, u32[]{:S(2)}) async-start(bf16[2,448,2048]{1,0,2:T(2,128)(2,1)} %bitcast.88), calls=%async_computation.1 | async-start | bytes 8388608 | tf_op jit(solution)/shard_map/all_to_all | solution.py:72
  94.9 220.5 %all-gather.3.cloned.1.call-start = ((), (), s32[]{:S(2)}) async-start(), calls=%async_computation.3 | async-start | bytes 4587520 | tf_op jit(solution)/shard_map/all_gather | solution.py:97
  380.1 43.3 %all-to-all-start = ((bf16[8,2,57344]{2,1,0:T(2,128)(2,1)}), bf16[8,2,57344]{2,1,0:T(2,128)(2,1)S(1)}, u32[]{:S(2)}, u32[]{:S(2)}) async-start(bf16[8,2,57344]{2,1,0:T(2,128)(2,1)} %reshape.75), calls=%async_computation | async-start | bytes 3670016 | tf_op jit(solution)/shard_map/all_to_all | solution.py:101
  434.0 2.6 copy-start.2
  436.6 3.1 copy-start.1
Sparse Core Ops, SparseCore 0:
  75.2 207.9 reduce-scatter.3
  284.8 30.5 all-gather.2
